TPU v7x, 8 devices: a whole 2x2x1 slice. The times are simulated.
8 devices in a mesh: dp: 2 (over z, y), cp: 4 (over x, core).
Axes of the slice: x: 2, y: 2, z: 1, core: 2. Of those that a mesh axis runs over, the one named last changes fastest.
Arguments:
- hidden_states: bfloat16 [32, 128, 2048], P('dp', 'cp')
- norm_gain: float32 [2048], replicated
- w_gate: bfloat16 [2048, 11008], replicated
- w_up: bfloat16 [2048, 11008], replicated
- w_down: bfloat16 [11008, 2048], replicated
- final_gain: float32 [2048], replicated
- w_value: float32 [2048], replicated
- b_value: float32 [], replicated
- rewards: float32 [32, 128], P('dp', 'cp')
- mask: int32 [32, 128], P('dp', 'cp')
Outputs:
- output 1: float32 [32, 128], P('dp', 'cp')
- output 2: float32 [32, 128], P('dp', 'cp')
- output 3: float32 [32, 128], P('dp', 'cp')
All inputs are finite; a program needn't handle non-finite values.
Results may differ from a plain program's by a relative error of at most 0.001.
Values sent between devices are 32-bit elements.
A program may use at most 1 GiB of HBM per device.

v0:
```python
import math
import jax
import jax.numpy as jnp
from jax import lax
from jax.sharding import PartitionSpec as P

NORM_EPS = 1e-6
WHITEN_EPS = 1e-8
DISCOUNT = 1.0
GAE_LAMBDA = 0.995
LOG_DECAY = math.log(DISCOUNT * GAE_LAMBDA)


def critic_values(x_blk, norm_gain, w_gate, w_up, w_down, final_gain, w_value, b_value):
    x_f32 = x_blk.astype(jnp.float32)
    normed = (x_f32 * lax.rsqrt(jnp.mean(x_f32 * x_f32, axis=-1, keepdims=True) + NORM_EPS) * norm_gain).astype(jnp.bfloat16)
    gate = jnp.einsum('bsd,df->bsf', normed, w_gate, preferred_element_type=jnp.float32)
    up_val = jnp.einsum('bsd,df->bsf', normed, w_up, preferred_element_type=jnp.float32)
    hidden = (jax.nn.silu(gate) * up_val).astype(jnp.bfloat16)
    resid = x_f32 + jnp.einsum('bsf,fd->bsd', hidden, w_down, preferred_element_type=jnp.float32)
    resid_n = resid * lax.rsqrt(jnp.mean(resid * resid, axis=-1, keepdims=True) + NORM_EPS)
    return jnp.sum(resid_n * (final_gain * w_value), axis=-1) + b_value


def decay_matrix(seq_len):
    positions = jnp.arange(seq_len)
    gap = positions[:, None] - positions[None, :]
    return jnp.where(gap >= 0, jnp.exp(jnp.maximum(gap, 0).astype(jnp.float32) * LOG_DECAY), 0.0)


def tail_decay(seq_len):
    positions = jnp.arange(seq_len)
    return jnp.exp((seq_len - positions).astype(jnp.float32) * LOG_DECAY)


def solution(mesh):
    cp_size = mesh.shape['cp']
    left_perm = [(source, source - 1) for source in range(1, cp_size)]

    def local_step(x_blk, norm_gain, w_gate, w_up, w_down, final_gain, w_value, b_value, rew_blk, mask_blk):
        row_count, seq_len = rew_blk.shape
        mask_f = mask_blk.astype(jnp.float32)
        values = mask_f * critic_values(x_blk, norm_gain, w_gate, w_up, w_down, final_gain, w_value, b_value)
        next_first = lax.ppermute(values[:, 0], 'cp', left_perm)
        next_vals = jnp.concatenate([values[:, 1:], next_first[:, None]], axis=1)
        delta = mask_f * rew_blk + DISCOUNT * next_vals - values
        local_adv = jnp.dot(delta, decay_matrix(seq_len), precision=lax.Precision.HIGHEST)
        head_adv = local_adv[:, 0]
        piece_gain = math.exp(seq_len * LOG_DECAY)

        def carry_step(step_idx, carry):
            return lax.ppermute(head_adv + piece_gain * carry, 'cp', left_perm)

        carry_in = lax.fori_loop(0, cp_size - 1, carry_step, jnp.zeros((row_count,), jnp.float32))
        advantage = local_adv + carry_in[:, None] * tail_decay(seq_len)[None, :]
        local_sums = jnp.stack([jnp.sum(mask_f), jnp.sum(mask_f * advantage), jnp.sum(mask_f * advantage * advantage)])
        totals = lax.psum(local_sums, ('dp', 'cp'))
        mean_adv = totals[1] / totals[0]
        var_adv = totals[2] / totals[0] - mean_adv * mean_adv
        white = mask_f * (advantage - mean_adv) * lax.rsqrt(var_adv + WHITEN_EPS)
        return values, mask_f * (advantage + values), white

    tok_spec = P('dp', 'cp')
    in_specs = (P('dp', 'cp', None), P(None), P(None, None), P(None, None), P(None, None), P(None), P(None), P(), tok_spec, tok_spec)
    return jax.shard_map(local_step, mesh=mesh, in_specs=in_specs, out_specs=(tok_spec, tok_spec, tok_spec), check_vma=False)
```

profile of v0, /device:TPU:0, one launch (start us, length us, event | category | flops | bytes accessed | tf_op | source)
XLA Modules:
  0.0 157.2 jit_solution(17830540428079171557)
XLA Ops:
  0.6 2.1 %fusion.11 = f32[16,32]{1,0:T(8,128)S(1)} fusion(bf16[16,32,2048]{2,1,0:T(8,128)(2,1)} %param.12), kind=kLoop, calls=%fused_computation.12 | loop fusion | flops 3145216 | bytes 2099200 | tf_op jit(solution)/shard_map/reduce_sum | solution.py:16
  2.7 0.0 copy-start
  2.7 0.0 copy-start.6
  2.7 34.2 %fusion.4 = f32[16,32,11008]{2,1,0:T(8,128)} fusion(bf16[2048,11008]{1,0:T(8,128)(2,1)} %param.14, bf16[16,32,2048]{2,1,0:T(8,128)(2,1)} %param.12, f32[2048]{0:T(1024)} %param.13, f32[16,32]{1,0:T(8,128)S(1)} %add_rsqrt_fusion.1), kind=kOutput, calls=%fused_computation.5 | convolution fusion | flops 23089643520 | bytes 69740544 | tf_op jit(solution)/shard_map/bsd,df->bsf/dot_general | solution.py:17
  37.0 0.0 copy-done
  37.0 0.0 copy-done.6
  37.0 33.5 %multiply_convert_fusion.clone.3.clone.4 = bf16[16,32,11008]{2,1,0:T(8,128)(2,1)} fusion(f32[16,32,11008]{2,1,0:T(8,128)} %fusion.4, bf16[2048,11008]{1,0:T(8,128)(2,1)} %param.15, bf16[16,32,2048]{2,1,0:T(8,128)(2,1)S(1)} %copy-done, f32[2048]{0:T(1024)S(1)} %copy-done.6, f32[16,32]{1,0:T(8,128)S(1)} %add_rsqrt_fusion.1), kind=kOutput, calls=%fused_computation.7.clone.clone.clone.clone.clone.clone.clone.1 | convolution fusion | flops 23123460096 | bytes 81012736 | tf_op jit(solution)/shard_map/bsd,df->bsf/dot_general | solution.py:18
  70.4 0.0 copy-start.3
  70.4 0.0 copy-start.4
  70.4 32.8 %multiply_reduce_fusion.1 = (f32[16,32]{1,0:T(8,128)S(1)}, f32[16,32,2048]{2,1,0:T(8,128)}) fusion(bf16[11008,2048]{1,0:T(8,128)(2,1)} %param.16, bf16[16,32,2048]{2,1,0:T(8,128)(2,1)S(1)} %copy-done, bf16[16,32,11008]{2,1,0:T(8,128)(2,1)} %multiply_convert_fusion.clone.3.clone.4), kind=kOutput, calls=%fused_computation.16 | convolution fusion | flops 23089643520 | bytes 62654464 | tf_op jit(solution)/shard_map/bsf,fd->bsd/dot_general | solution.py:20
  103.2 0.0 copy-start.2
  103.2 0.0 copy-start.5
  103.9 0.0 copy-done.3
  103.9 0.0 copy-done.4
  103.9 2.8 %multiply_reduce_fusion = f32[16,32]{1,0:T(8,128)S(1)} fusion(f32[16,32,2048]{2,1,0:T(8,128)} %get-tuple-element.36, f32[2048]{0:T(1024)S(1)} %mul.118, f32[16,32]{1,0:T(8,128)S(1)} %add_rsqrt_fusion), kind=kLoop, calls=%fused_computation.15 | loop fusion | flops 3145216 | bytes 4206592 | tf_op jit(solution)/shard_map/reduce_sum | solution.py:22
  106.7 0.0 copy-done.2
  106.7 0.0 copy-start.1
  106.7 0.1 slice_reduce_fusion.1
  106.8 1.3 collective-permute-start.1
  108.1 0.1 slice.25
  108.2 2.0 %collective-permute-done.1 = f32[16]{0:T(128)S(1)} collective-permute-done((f32[16]{0:T(128)S(1)}, f32[16]{0:T(128)S(1)}, u32[]{:S(2)}, u32[]{:S(2)}) %collective-permute-start.1) | collective-permute-done | bytes 96 | tf_op jit(solution)/shard_map/ppermute | solution.py:44
  110.2 0.1 copy.14
  110.3 0.0 copy-done.5
  110.3 0.2 fusion.24
  110.5 0.1 slice_reduce_fusion
  110.6 15.6 %while.10 = (s32[]{:T(128)}, f32[16]{0:T(128)S(1)}, f32[16]{0:T(128)S(1)}, s32[]{:T(128)}) while((s32[]{:T(128)}, f32[16]{0:T(128)S(1)}, f32[16]{0:T(128)S(1)}, s32[]{:T(128)}) %tuple.29), condition=%wide.region_4.5_spmd, body=%wide.region_3.4_spmd.sunk | while | flops 34 | bytes 541 | solution.py:54
  110.7 1.3 collective-permute-start
  112.0 4.5 %collective-permute-done = f32[16]{0:T(128)S(1)} collective-permute-done((f32[16]{0:T(128)S(1)}, f32[16]{0:T(128)S(1)}, u32[]{:S(2)}, u32[]{:S(2)}) %collective-permute-start) | collective-permute-done | bytes 96 | tf_op jit(solution)/shard_map/while/body/eval_jaxpr/ppermute | solution.py:52
  116.4 1.3 collective-permute-start
  117.7 3.6 %collective-permute-done = f32[16]{0:T(128)S(1)} collective-permute-done((f32[16]{0:T(128)S(1)}, f32[16]{0:T(128)S(1)}, u32[]{:S(2)}, u32[]{:S(2)}) %collective-permute-start) | collective-permute-done | bytes 96 | tf_op jit(solution)/shard_map/while/body/eval_jaxpr/ppermute | solution.py:52
  121.3 1.3 collective-permute-start
  122.6 3.6 %collective-permute-done = f32[16]{0:T(128)S(1)} collective-permute-done((f32[16]{0:T(128)S(1)}, f32[16]{0:T(128)S(1)}, u32[]{:S(2)}, u32[]{:S(2)}) %collective-permute-start) | collective-permute-done | bytes 96 | tf_op jit(solution)/shard_map/while/body/eval_jaxpr/ppermute | solution.py:52
  126.2 0.8 fusion.41
  127.0 2.1 %pad_maximum_fusion = f32[3]{0:T(128)S(1)} fusion(f32[1]{0:T(128)} %bitcast.6, f32[1]{0:T(128)} %bitcast.5, f32[1]{0:T(128)} %bitcast.4), kind=kLoop, calls=%fused_computation.48 | loop fusion | flops 6 | bytes 24 | tf_op jit(solution)/shard_map/stack | solution.py:56
  129.0 24.0 %psum.7 = f32[3]{0:T(128)S(1)} all-reduce(f32[3]{0:T(128)S(1)} %pad_maximum_fusion), channel_id=1, replica_groups=mesh['dp'=2,'cp'=4] {'dp','cp'}, use_global_device_ids=true, to_apply=%region_8.9 | all-reduce | flops 3 | bytes 24 | tf_op jit(solution)/shard_map/psum | solution.py:57
  153.0 0.7 fusion.47
  156.5 0.7 multiply_multiply_fusion
  157.2 0.0 copy-done.1
  (9 shorter events, 0.0 us)
Async XLA Ops:
  2.7 34.3 %copy-start = (bf16[16,32,2048]{2,1,0:T(8,128)(2,1)S(1)}, bf16[16,32,2048]{2,1,0:T(8,128)(2,1)}, u32[]{:S(2)}) copy-start(bf16[16,32,2048]{2,1,0:T(8,128)(2,1)} %param.12) | copy-start | bytes 6291460
  2.7 34.3 %copy-start.6 = (f32[2048]{0:T(1024)S(1)}, f32[2048]{0:T(1024)}, u32[]{:S(2)}) copy-start(f32[2048]{0:T(1024)} %param.13) | copy-start | bytes 24580
  70.4 33.5 %copy-start.3 = (f32[2048]{0:T(1024)S(1)}, f32[2048]{0:T(1024)}, u32[]{:S(2)}) copy-start(f32[2048]{0:T(1024)} %param.17) | copy-start | bytes 24580
  70.4 33.5 %copy-start.4 = (f32[2048]{0:T(1024)S(1)}, f32[2048]{0:T(1024)}, u32[]{:S(2)}) copy-start(f32[2048]{0:T(1024)} %param.18) | copy-start | bytes 24580
  103.2 3.5 %copy-start.2 = (s32[16,32]{1,0:T(8,128)S(1)}, s32[16,32]{1,0:T(8,128)}, u32[]{:S(2)}) copy-start(s32[16,32]{1,0:T(8,128)} %param.21) | copy-start | bytes 6148
  103.2 7.1 %copy-start.5 = (f32[16,32]{1,0:T(8,128)S(1)}, f32[16,32]{1,0:T(8,128)}, u32[]{:S(2)}) copy-start(f32[16,32]{1,0:T(8,128)} %param.20) | copy-start | bytes 6148
  106.7 50.5 %copy-start.1 = (f32[16,32]{1,0:T(8,128)}, f32[16,32]{1,0:T(8,128)S(1)}, u32[]{:S(2)}) copy-start(f32[16,32]{1,0:T(8,128)S(1)} %add_multiply_fusion.1) | copy-start | bytes 6148
  106.8 3.4 %collective-permute-start.1 = (f32[16]{0:T(128)S(1)}, f32[16]{0:T(128)S(1)}, u32[]{:S(2)}, u32[]{:S(2)}) collective-permute-start(f32[16]{0:T(128)S(1)} %slice_reduce_fusion.1), channel_id=1, source_target_pairs={{1,0},{2,1},{3,2},{5,4},{6,5},{7,6}} | collective-permute-start | bytes 200 | tf_op jit(solution)/shard_map/ppermute | solution.py:44
  110.7 5.8 %collective-permute-start = (f32[16]{0:T(128)S(1)}, f32[16]{0:T(128)S(1)}, u32[]{:S(2)}, u32[]{:S(2)}) collective-permute-start(f32[16]{0:T(128)S(1)} %multiply_add_fusion.3), channel_id=1, source_target_pairs={{1,0},{2,1},{3,2},{5,4},{6,5},{7,6}} | collective-permute-start | bytes 200 | tf_op jit(solution)/shard_map/while/body/eval_jaxpr/ppermute | solution.py:52
  116.4 4.9 %collective-permute-start = (f32[16]{0:T(128)S(1)}, f32[16]{0:T(128)S(1)}, u32[]{:S(2)}, u32[]{:S(2)}) collective-permute-start(f32[16]{0:T(128)S(1)} %multiply_add_fusion.3), channel_id=1, source_target_pairs={{1,0},{2,1},{3,2},{5,4},{6,5},{7,6}} | collective-permute-start | bytes 200 | tf_op jit(solution)/shard_map/while/body/eval_jaxpr/ppermute | solution.py:52
  121.3 4.9 %collective-permute-start = (f32[16]{0:T(128)S(1)}, f32[16]{0:T(128)S(1)}, u32[]{:S(2)}, u32[]{:S(2)}) collective-permute-start(f32[16]{0:T(128)S(1)} %multiply_add_fusion.3), channel_id=1, source_target_pairs={{1,0},{2,1},{3,2},{5,4},{6,5},{7,6}} | collective-permute-start | bytes 200 | tf_op jit(solution)/shard_map/while/body/eval_jaxpr/ppermute | solution.py:52
where the time goes:
time: 158 us; the launch traced here: 157 us
  matrix products  101 us (64%)
  blocking collectives  24 us (15%)
  waiting for transfers between devices  13.7 us (9%)
  other arithmetic  8.37 us (5%)
  starting transfers between devices  5.14 us (3%)
  between operations  4.18 us (3%)
    dot_general x1, matrix products, critic_values(): jnp.einsum('bsd,df->bsf', normed, w_gate, preferred_element_type=jnp.floa...  34.2 us
    dot_general x1, matrix products, critic_values(): jnp.einsum('bsd,df->bsf', normed, w_up, preferred_element_type=jnp.float32)  33.5 us
    dot_general x1, matrix products, critic_values(): jnp.einsum('bsf,fd->bsd', hidden, w_down, preferred_element_type=jnp.floa...  32.8 us
    psum x1, blocking collectives, local_step(): totals = lax.psum(local_sums, ('dp', 'cp'))  24 us
    ppermute x3, waiting for transfers between devices, carry_step(): return lax.ppermute(head_adv + piece_gain * carry, 'cp', left_perm)  11.6 us
    ppermute x3, starting transfers between devices, carry_step(): return lax.ppermute(head_adv + piece_gain * carry, 'cp', left_perm)  3.85 us
  transfers between devices with their start and end apart: 4, of which 4 were waited for; matrix products, arithmetic and copies ran while one was open for 0% of the time, Pallas kernels for 0%

commit v1 on v0

v1 whole, which is shorter than its diff:
```python
import functools
import math

import jax
import jax.numpy as jnp
from jax import lax
from jax.experimental import pallas as pl
from jax.experimental.pallas import tpu as pltpu
from jax.sharding import PartitionSpec as P

NORM_EPS = 1e-6
WHITEN_EPS = 1e-8
DISCOUNT = 1.0
GAE_LAMBDA = 0.995
MESH = pl.DeviceIdType.MESH

ROWS, PIECE, CP, DP = 16, 32, 4, 2
SEQ = PIECE * CP
TOK = ROWS * PIECE
HALF = TOK // 2
SEND_CHUNKS = 4
FC = 256
SLOTS = 8
VARIANTS = (192, 224, 256, 288, 320, 384, 448, 512)


def iota(shape, dim):
    return lax.broadcasted_iota(jnp.int32, shape, dim)


def everyone(dp, cp):
    for step in range(1, DP * CP):
        yield lax.rem(dp + step // CP, DP), lax.rem(cp + step % CP, CP)


def token_row(placed):
    spread = (lax.rem(iota((SEQ, TOK), 0), PIECE) == lax.rem(iota((SEQ, TOK), 1), PIECE)).astype(jnp.bfloat16)
    by_row = jnp.dot(placed.astype(jnp.bfloat16), spread, preferred_element_type=jnp.float32)
    own = iota((ROWS, TOK), 0) == iota((ROWS, TOK), 1) // PIECE
    return jnp.sum(jnp.where(own, by_row, 0.0), axis=0, keepdims=True)


def token_rank(row):
    upper = (iota((TOK, TOK), 0) <= iota((TOK, TOK), 1)).astype(jnp.bfloat16)
    upto = jnp.dot(jnp.broadcast_to(row, (8, TOK)).astype(jnp.bfloat16), upper, preferred_element_type=jnp.float32)[:1]
    return jnp.where(row > 0.0, upto - 1.0, -1.0)


def gather_kernel(x_hbm, mask_ref, rew_ref, xs_ref, tid_ref, cnt_ref, gm_ref,
                  x_v, sendbuf, recvbuf, pack, packs, place, x_sem, pk_send, pk_recv, x_send, x_recv):
    dp, cp = lax.axis_index('dp'), lax.axis_index('cp')
    mate = cp + 1 - 2 * lax.rem(cp, 2)
    load = pltpu.make_async_copy(x_hbm, x_v, x_sem)
    load.start()
    barrier = pltpu.get_barrier_semaphore()
    for to in everyone(dp, cp):
        pl.semaphore_signal(barrier, inc=1, device_id=to, device_id_type=MESH)

    mask_f = mask_ref[...].astype(jnp.float32)
    for half, block in enumerate((mask_f, jnp.where(mask_f > 0.0, rew_ref[...], 0.0))):
        place[half] = jnp.zeros((ROWS, SEQ), jnp.float32)
        place[half, :, :PIECE] = block
        base = place[half]
        moved = base
        for piece in range(1, CP):
            moved = jnp.where(cp == piece, pltpu.roll(base, piece * PIECE, 1), moved)
        pack[half] = moved
    row = token_row(pack[0])
    rank = token_rank(row)
    pl.semaphore_wait(barrier, DP * CP - 1)

    me = dp * CP + cp
    shares = []
    for k, to in enumerate(everyone(dp, cp)):
        share = pltpu.make_async_remote_copy(
            src_ref=pack, dst_ref=packs.at[k], send_sem=pk_send.at[k], recv_sem=pk_recv.at[k],
            device_id=to, device_id_type=MESH)
        share.start()
        shares.append(share)

    load.wait()
    send_rank = (2 * iota((HALF, TOK), 0) + 1).astype(jnp.float32)
    pick = (rank == send_rank).astype(jnp.bfloat16)
    width = x_v.shape[1] // SEND_CHUNKS
    moves = []
    for j in range(SEND_CHUNKS):
        cols = slice(j * width, (j + 1) * width)
        sendbuf[j] = jnp.dot(pick, x_v[:, cols], preferred_element_type=jnp.float32)
        move = pltpu.make_async_remote_copy(
            src_ref=sendbuf.at[j], dst_ref=recvbuf.at[j], send_sem=x_send.at[j], recv_sem=x_recv.at[j],
            device_id=(dp, mate), device_id_type=MESH)
        move.start()
        moves.append(move)

    for share in shares:
        share.wait_recv()
    placed = [[pack[half] for half in range(2)]] + [[packs[k, half] for half in range(2)] for k in range(DP * CP - 1)]
    same = [sum(placed[k][half] for k in range(CP)) for half in range(2)]
    other = [sum(placed[k][half] for k in range(CP, 2 * CP)) for half in range(2)]
    for half in range(2):
        gm_ref[half, :ROWS, :] = same[half]
        gm_ref[half, ROWS:, :] = other[half]
    lane = iota((ROWS, SEQ), 1)
    mate_row = token_row(jnp.where(lane // PIECE == mate, same[0], 0.0))
    mate_rank = token_rank(mate_row)
    got = jnp.floor(jnp.sum(mate_row, axis=1, keepdims=True) * 0.5)
    keep = jnp.floor((jnp.sum(row, axis=1, keepdims=True) + 1.0) * 0.5)
    cnt_ref[...] = jnp.broadcast_to(got + keep, (8, 128))

    slot = iota((TOK, TOK), 0).astype(jnp.float32)
    own = rank == 2.0 * (slot - got)
    own = jnp.logical_and(own, slot >= got)
    tok = iota((1, TOK), 1)
    code = ((tok // PIECE) * SEQ + lax.rem(tok, PIECE)).astype(jnp.float32)
    own_code = code + (cp * PIECE).astype(jnp.float32)
    mate_code = code + (mate * PIECE).astype(jnp.float32)
    theirs = mate_rank == send_rank
    tid = jnp.sum(jnp.where(own, own_code, 0.0), axis=1, keepdims=True)
    tid_ref[...] = tid.astype(jnp.int32)
    tid_ref[:HALF, :] = (tid[:HALF] + jnp.sum(jnp.where(theirs, mate_code, 0.0), axis=1, keepdims=True)).astype(jnp.int32)
    own_pick = own.astype(jnp.bfloat16)
    came = iota((HALF, width), 0).astype(jnp.float32) < got
    for j in range(SEND_CHUNKS):
        cols = slice(j * width, (j + 1) * width)
        xs_ref[:, cols] = jnp.dot(own_pick, x_v[:, cols], preferred_element_type=jnp.float32).astype(jnp.bfloat16)
    for j in range(SEND_CHUNKS):
        cols = slice(j * width, (j + 1) * width)
        moves[j].wait_recv()
        xs_ref[:HALF, cols] = jnp.where(came, recvbuf[j], xs_ref[:HALF, cols].astype(jnp.float32)).astype(jnp.bfloat16)
    for share in shares:
        share.wait_send()
    for move in moves:
        move.wait_send()


def mlp_kernel(cnt_ref, xs_ref, tid_ref, gain_ref, head_ref, bv_ref, wg_hbm, wu_hbm, wd_hbm, out_ref,
               wg_buf, wu_buf, wd_buf, xn, acc, inner, col, sems):
    model = xs_ref.shape[1]
    chunks = wd_hbm.shape[0] // FC

    def copies(i, which=(0, 1, 2)):
        slot = lax.rem(i, SLOTS)
        at = pl.ds(pl.multiple_of(i * FC, FC), FC)
        make = (lambda: pltpu.make_async_copy(wg_hbm.at[:, at], wg_buf.at[slot], sems.at[0, slot]),
                lambda: pltpu.make_async_copy(wu_hbm.at[:, at], wu_buf.at[slot], sems.at[1, slot]),
                lambda: pltpu.make_async_copy(wd_hbm.at[at, :], wd_buf.at[slot], sems.at[2, slot]))
        return [make[w]() for w in which]

    def wait(i):
        for copy in copies(i):
            copy.wait()

    def refill(i):
        @pl.when(i + SLOTS < chunks)
        def _():
            for copy in copies(i + SLOTS):
                copy.start()

    for i in range(SLOTS):
        for copy in copies(jnp.int32(i)):
            copy.start()
    count = jnp.max(cnt_ref[...]).astype(jnp.int32)

    blocks = (count + 31) // 32

    def norm(b, _):
        rows = pl.ds(pl.multiple_of(b * 32, 32), 32)
        x = xs_ref[rows, :].astype(jnp.float32)
        scale = lax.rsqrt(jnp.mean(x * x, axis=-1, keepdims=True) + NORM_EPS)
        xn[rows, :] = (x * scale * gain_ref[...]).astype(jnp.bfloat16)
        return 0

    lax.fori_loop(0, blocks, norm, 0)

    def run(size):
        def inside(i, where):
            slot = lax.rem(i, SLOTS)
            gate = jnp.dot(xn[:size, :], wg_buf[slot], preferred_element_type=jnp.float32)
            up = jnp.dot(xn[:size, :], wu_buf[slot], preferred_element_type=jnp.float32)
            inner[:size, where * FC:(where + 1) * FC] = (jax.nn.silu(gate) * up).astype(jnp.bfloat16)

        def down(i, where):
            return jnp.dot(inner[:size, where * FC:(where + 1) * FC], wd_buf[lax.rem(i, SLOTS)],
                           preferred_element_type=jnp.float32)

        wait(jnp.int32(0))
        inside(jnp.int32(0), 0)
        acc[:size, :] = down(jnp.int32(0), 0)

        def body(j, _):
            first, second = 2 * j + 1, 2 * j + 2
            wait(first)
            wait(second)
            refill(first - 1)
            @pl.when(j > 0)
            def _():
                refill(first - 2)
            inside(first, 0)
            inside(second, 1)
            acc[:size, :] += down(first, 0) + down(second, 1)
            return 0

        lax.fori_loop(0, (chunks - 1) // 2, body, 0)

    for k, size in enumerate(VARIANTS):
        above = VARIANTS[k - 1] if k else -1
        @pl.when(jnp.logical_and(count > above, count <= size))
        def _():
            run(size)

    col[...] = jnp.zeros_like(col)

    def head(b, _):
        rows = pl.ds(pl.multiple_of(b * 32, 32), 32)
        h = xs_ref[rows, :].astype(jnp.float32) + acc[rows, :]
        scale = lax.rsqrt(jnp.mean(h * h, axis=-1, keepdims=True) + NORM_EPS)
        val = jnp.sum(h * head_ref[...], axis=-1, keepdims=True) * scale + bv_ref[0]
        val = jnp.where(iota((32, 1), 0) + b * 32 < count, val, 0.0)
        col[rows, :] = jnp.broadcast_to(val, (32, SEQ))
        return 0

    lax.fori_loop(0, blocks, head, 0)
    at_row = (tid_ref[...] // SEQ == iota((TOK, ROWS), 1)).astype(jnp.float32)
    at_lane = jnp.where(lax.rem(tid_ref[...], SEQ) == iota((TOK, SEQ), 1), col[...], 0.0)
    out_ref[...] = lax.dot_general(at_row, at_lane, (((0,), (0,)), ((), ())), precision=lax.Precision.HIGHEST,
                                   preferred_element_type=jnp.float32)


def gae_kernel(vals_ref, gm_ref, v_ref, ret_ref, white_ref, came, send, recv):
    dp, cp = lax.axis_index('dp'), lax.axis_index('cp')
    barrier = pltpu.get_barrier_semaphore()
    for to in everyone(dp, cp):
        pl.semaphore_signal(barrier, inc=1, device_id=to, device_id_type=MESH)
    pl.semaphore_wait(barrier, DP * CP - 1)
    shares = []
    for k, to in enumerate(everyone(dp, cp)):
        share = pltpu.make_async_remote_copy(
            src_ref=vals_ref, dst_ref=came.at[k], send_sem=send.at[k], recv_sem=recv.at[k],
            device_id=to, device_id_type=MESH)
        share.start()
        shares.append(share)
    for share in shares:
        share.wait_recv()
    same = vals_ref[...] + came[0] + came[1] + came[2]
    other = came[3] + came[4] + came[5] + came[6]
    values = jnp.concatenate([same, other], axis=0)
    mask, rew = gm_ref[0], gm_ref[1]
    lane = iota((2 * ROWS, SEQ), 1)

    def ahead(z, step):
        return jnp.where(lane < SEQ - step, pltpu.roll(z, SEQ - step, 1), 0.0)

    adv = rew + DISCOUNT * ahead(values, 1) - values
    step = 1
    while step < SEQ:
        adv = adv + math.pow(DISCOUNT * GAE_LAMBDA, step) * ahead(adv, step)
        step *= 2

    def total(z):
        return jnp.sum(jnp.sum(z, axis=0, keepdims=True), axis=1, keepdims=True)

    count = total(mask)
    mean = total(mask * adv) / count
    var = total(mask * adv * adv) / count - mean * mean
    white = mask * (adv - mean) * lax.rsqrt(var + WHITEN_EPS)
    for out, z in ((v_ref, values), (ret_ref, mask * (adv + values)), (white_ref, white)):
        mine = z[:ROWS]
        moved = mine
        for piece in range(1, CP):
            moved = jnp.where(cp == piece, pltpu.roll(mine, SEQ - piece * PIECE, 1), moved)
        out[...] = moved[:, :PIECE]
    for share in shares:
        share.wait_send()


def vmem():
    return pl.BlockSpec(memory_space=pltpu.VMEM)


def smem():
    return pl.BlockSpec(memory_space=pltpu.SMEM)


def hbm():
    return pl.BlockSpec(memory_space=pl.ANY)


def solution(mesh):
    def local_step(x_blk, norm_gain, w_gate, w_up, w_down, final_gain, w_value, b_value, rew_blk, mask_blk):
        rows, piece, model = x_blk.shape
        f32, bf16 = jnp.float32, jnp.bfloat16
        x = x_blk.reshape(TOK, model)
        width = model // SEND_CHUNKS
        xs, tid, cnt, gm = pl.pallas_call(
            gather_kernel,
            name='gather_tokens',
            out_shape=(jax.ShapeDtypeStruct((TOK, model), bf16), jax.ShapeDtypeStruct((TOK, 1), jnp.int32),
                       jax.ShapeDtypeStruct((8, 128), f32), jax.ShapeDtypeStruct((2, DP * ROWS, SEQ), f32)),
            in_specs=[hbm(), vmem(), vmem()],
            out_specs=(vmem(),) * 4,
            scratch_shapes=[
                pltpu.VMEM((TOK, model), bf16),
                pltpu.VMEM((SEND_CHUNKS, HALF, width), f32), pltpu.VMEM((SEND_CHUNKS, HALF, width), f32),
                pltpu.VMEM((2, ROWS, SEQ), f32), pltpu.VMEM((DP * CP - 1, 2, ROWS, SEQ), f32),
                pltpu.VMEM((2, ROWS, SEQ), f32),
                pltpu.SemaphoreType.DMA,
                pltpu.SemaphoreType.DMA((DP * CP - 1,)), pltpu.SemaphoreType.DMA((DP * CP - 1,)),
                pltpu.SemaphoreType.DMA((SEND_CHUNKS,)), pltpu.SemaphoreType.DMA((SEND_CHUNKS,)),
            ],
            compiler_params=pltpu.CompilerParams(collective_id=0, has_side_effects=True, vmem_limit_bytes=40 << 20),
        )(x, mask_blk, rew_blk)
        vals = pl.pallas_call(
            mlp_kernel,
            name='active_mlp',
            out_shape=jax.ShapeDtypeStruct((ROWS, SEQ), f32),
            in_specs=[vmem(), vmem(), vmem(), vmem(), vmem(), smem(), hbm(), hbm(), hbm()],
            out_specs=vmem(),
            scratch_shapes=[
                pltpu.VMEM((SLOTS, model, FC), bf16), pltpu.VMEM((SLOTS, model, FC), bf16),
                pltpu.VMEM((SLOTS, FC, model), bf16),
                pltpu.VMEM((TOK, model), bf16), pltpu.VMEM((TOK, model), f32), pltpu.VMEM((TOK, 2 * FC), bf16),
                pltpu.VMEM((TOK, SEQ), f32),
                pltpu.SemaphoreType.DMA((3, SLOTS)),
            ],
            compiler_params=pltpu.CompilerParams(vmem_limit_bytes=60 << 20),
        )(cnt, xs, tid, norm_gain.reshape(1, model), (final_gain * w_value).reshape(1, model), b_value.reshape(1),
          w_gate, w_up, w_down)
        block = jax.ShapeDtypeStruct((rows, piece), f32)
        return pl.pallas_call(
            gae_kernel,
            name='gae',
            out_shape=(block, block, block),
            in_specs=[vmem(), vmem()],
            out_specs=(vmem(),) * 3,
            scratch_shapes=[
                pltpu.VMEM((DP * CP - 1, ROWS, SEQ), f32),
                pltpu.SemaphoreType.DMA((DP * CP - 1,)), pltpu.SemaphoreType.DMA((DP * CP - 1,)),
            ],
            compiler_params=pltpu.CompilerParams(collective_id=1, has_side_effects=True),
        )(vals, gm)

    tok_spec = P('dp', 'cp')
    in_specs = (P('dp', 'cp', None), P(None), P(None, None), P(None, None), P(None, None), P(None), P(None), P(),
                tok_spec, tok_spec)
    return jax.shard_map(local_step, mesh=mesh, in_specs=in_specs, out_specs=(tok_spec,) * 3, check_vma=False)
```

time: 158 us -> 76.7 us (0.49)
  matrix products: 101 us -> 0 us
  Pallas kernels: 0 us -> 63.2 us
  blocking collectives: 24 us -> 0 us
  waiting for transfers between devices: 13.7 us -> 0 us
  local copies, waits for them, and re-layouts: 1.08 us -> 10.1 us
  other arithmetic: 8.37 us -> 1.31 us
  starting transfers between devices: 5.14 us -> 0 us
  between operations: 4.18 us -> 1.32 us
    dot_general x4 -> x0, matrix products: 101 us -> none  [the longest x1 34.2 us: critic_values(): jnp.einsum('bsd,df->bsf', normed, w_gate, preferred_element_type=jnp.floa...]
    pallas_call x0 -> x3, Pallas kernels: none -> 63.2 us  [the longest x1 46.6 us: local_step(): pl.pallas_call(mlp_kernel, name='active_mlp', out_shape=jax.ShapeDtypeStr...]
    psum x1 -> x0, blocking collectives: 24 us -> none  [local_step(): totals = lax.psum(local_sums, ('dp', 'cp'))]
    ppermute x4 -> x0, waiting for transfers between devices: 13.7 us -> none  [the longest x3 11.6 us: carry_step(): return lax.ppermute(head_adv + piece_gain * carry, 'cp', left_perm)]
    unnamed x14 -> x17, local copies, waits for them, and re-layouts: 0.03 us -> 10.1 us
    reduce_sum x3 -> x0, other arithmetic: 5.59 us -> none  [the longest x1 2.75 us: critic_values(): return jnp.sum(resid_n * (final_gain * w_value), axis=-1) + b_value]
    ppermute x4 -> x0, starting transfers between devices: 5.14 us -> none  [the longest x3 3.85 us: carry_step(): return lax.ppermute(head_adv + piece_gain * carry, 'cp', left_perm)]
    another operation x1 -> x0, other arithmetic: 2.05 us -> none  [local_step(): jnp.stack([jnp.sum(mask_f), jnp.sum(mask_f * advantage), jnp.sum(mask_f *...]
  transfers between devices with their start and end apart: 4 -> 0, of which waited for: 4 -> 0; matrix products, arithmetic and copies ran while one was open for 0% -> 0% of each run, Pallas kernels for 0% -> 0%
where the time goes in v1:
time: 76.7 us; the launch traced here: 76 us
  Pallas kernels  63.2 us (82%)
  local copies, waits for them, and re-layouts  10.1 us (13%)
  between operations  1.32 us (2%)
  other arithmetic  1.31 us (2%)
    pallas_call x1, Pallas kernels, local_step(): pl.pallas_call(mlp_kernel, name='active_mlp', out_shape=jax.ShapeDtypeStr...  46.6 us
    unnamed x17, local copies, waits for them, and re-layouts  10.1 us
    pallas_call x1, Pallas kernels, local_step(): pl.pallas_call(gather_kernel, name='gather_tokens', out_shape=(jax.ShapeD...  9.21 us
    pallas_call x1, Pallas kernels, local_step(): pl.pallas_call(gae_kernel, name='gae', out_shape=(block, block, block), i...  7.49 us

profile of v1, /device:TPU:0, one launch (start us, length us, event | category | flops | bytes accessed | tf_op | source)
XLA Modules:
  0.0 76.0 jit_solution(6205801261186890185)
XLA Ops:
  1.3 1.3 %mul.3 = f32[2048]{0:T(1024)} multiply(f32[2048]{0:T(1024)} %param.15, f32[2048]{0:T(1024)} %param.16) | non-fusion elementwise | flops 2048 | bytes 24576 | tf_op jit(solution)/shard_map/mul | solution.py:326
  2.6 0.0 copy-start.1
  2.6 1.6 %copy-done.1 = bf16[16,32,2048]{2,1,0:T(8,128)(2,1)S(1)} copy-done((bf16[16,32,2048]{2,1,0:T(8,128)(2,1)S(1)}, bf16[16,32,2048]{2,1,0:T(8,128)(2,1)}, u32[]{:S(2)}) %copy-start.1) | copy-done | bytes 2097176
  4.2 0.0 copy-start.4
  4.2 0.7 copy-done.4
  4.9 0.0 copy-start.5
  4.9 0.7 copy-done.5
  5.6 9.2 %gather_tokens.1 = (bf16[512,2048]{1,0:T(8,128)(2,1)S(1)}, s32[512,1]{1,0:T(8,128)S(1)}, f32[8,128]{1,0:T(8,128)S(1)}, f32[2,32,128]{2,1,0:T(8,128)S(1)}) custom-call(bf16[512,2048]{1,0:T(8,128)(2,1)S(1)} %bitcast.5, s32[16,32]{1,0:T(8,128)S(1)} %copy-done.4, f32[16,32]{1,0:T(8,128)S(1)} %copy-done.5), custom_call_target="tpu_custom_call" | custom-call | tf_op jit(solution)/shard_map/gather_tokens/pallas_call | solution.py:294
  14.8 0.0 copy-start
  14.8 1.3 %copy-done = bf16[512,2048]{1,0:T(8,128)(2,1)} copy-done((bf16[512,2048]{1,0:T(8,128)(2,1)}, bf16[512,2048]{1,0:T(8,128)(2,1)S(1)}, u32[]{:S(2)}) %copy-start) | copy-done | bytes 2097176
  16.1 0.0 copy-start.2
  16.1 0.7 copy-done.2
  16.8 0.0 copy-start.3
  16.8 0.6 copy-done.3
  17.4 0.0 copy-start.6
  17.5 0.6 copy-done.6
  18.0 46.6 %active_mlp.1.vals_ref = f32[16,128]{1,0:T(8,128)} custom-call(f32[8,128]{1,0:T(8,128)} %copy-done.6, bf16[512,2048]{1,0:T(8,128)(2,1)} %copy-done, s32[512,1]{1,0:T(8,128)} %copy-done.2, f32[1,2048]{1,0:T(1,128)} %bitcast.7, f32[1,2048]{1,0:T(1,128)} %bitcast.6, f32[1]{0:T(128)} %bitcast.4.bv_ref, bf16[2048,11008]{1,0:T(8,128)(2,1)} %wg_hbm.1, ...), custom_call_target="tpu_custom_call" | custom-call | tf_op jit(solution)/shard_map/active_mlp/pallas_call | solution.py:312
  64.6 7.5 %gae.1 = (f32[16,32]{1,0:T(8,128)}, f32[16,32]{1,0:T(8,128)}, f32[16,32]{1,0:T(8,128)}) custom-call(f32[16,128]{1,0:T(8,128)} %active_mlp.1.vals_ref, f32[2,32,128]{2,1,0:T(8,128)} %copy-done.3), custom_call_target="tpu_custom_call" | custom-call | tf_op jit(solution)/shard_map/gae/pallas_call | solution.py:329
  72.1 1.3 %copy.17 = f32[16,32]{1,0:T(8,128)} copy(f32[16,32]{1,0:T(8,128)} %get-tuple-element.14) | data formatting | bytes 4096
  73.4 1.3 %copy.18 = f32[16,32]{1,0:T(8,128)} copy(f32[16,32]{1,0:T(8,128)} %get-tuple-element.15) | data formatting | bytes 4096
  74.7 1.3 %copy.19 = f32[16,32]{1,0:T(8,128)} copy(f32[16,32]{1,0:T(8,128)} %get-tuple-element.16) | data formatting | bytes 4096
Async XLA Ops:
  2.6 1.6 %copy-start.1 = (bf16[16,32,2048]{2,1,0:T(8,128)(2,1)S(1)}, bf16[16,32,2048]{2,1,0:T(8,128)(2,1)}, u32[]{:S(2)}) copy-start(bf16[16,32,2048]{2,1,0:T(8,128)(2,1)} %param.10) | copy-start | bytes 6291460
  4.2 0.7 copy-start.4
  4.9 0.7 copy-start.5
  14.8 1.3 %copy-start = (bf16[512,2048]{1,0:T(8,128)(2,1)}, bf16[512,2048]{1,0:T(8,128)(2,1)S(1)}, u32[]{:S(2)}) copy-start(bf16[512,2048]{1,0:T(8,128)(2,1)S(1)} %get-tuple-element.8.xs_ref) | copy-start | bytes 6291460
  16.1 0.7 copy-start.2
  16.8 0.6 copy-start.3
  17.4 0.6 copy-start.6
